TPU v7x, 32 devices: a whole 2x2x4 slice. The times are simulated.
32 devices in a mesh: strip: 4 (over z), tile: 8 (over y, x, core).
Axes of the slice: x: 2, y: 2, z: 4, core: 2. Of those that a mesh axis runs over, the one named last changes fastest.
Arguments:
- coords: float32 [1536, 3, 128], P(('strip', 'tile')), may hold values from -0.25 to 1536.25, as said below
- displacement: float32 [1536, 3, 128], P(('strip', 'tile')), may hold values from -0.75 to 0.75
- pairs: int32 [2048, 2], P(('strip', 'tile')), may hold values from 0 to 1535, as said below
- intact: int32 [2048, 128, 128], P(('strip', 'tile')), may hold values 0 or 1
Outputs:
- force: float32 [1536, 3, 128], P(('strip', 'tile'))
Inputs may be any that keep to these rules, and one draw needn't show every extreme that they name: `coords`: each point sits within 0.25 of its lattice site: tile t covers a 4 x 4 x 8 block of unit lattice sites starting at (4 (t // 384), 4 (t % 384), 0), point i at offset (i % 4, (i // 4) % 4, i // 16). `pairs`: the rows of one device (device number d = strip index * 8 + tile index) name as first tile one of the 48 tiles that this device holds, and as second tile a different one whose strip differs from the first's by at most one and whose place within its strip differs from the first's place within its strip by at most one.
All inputs are finite; a program needn't handle non-finite values. No bound on the sum of `intact` on one device may be relied on, other than what follows from the above.
Results may differ from a plain program's by a relative error of at most 0.0003.
Values sent between devices are 32-bit elements; how exact they have to be, the bound alone decides.
A program may use at most 64 MiB of HBM per device.

v0:
```python
import math

import jax
import jax.numpy as jnp
from jax import lax
from jax.experimental import pallas as pl
from jax.experimental.pallas import tpu as pltpu
from jax.sharding import PartitionSpec as P

horizon = 3.0
stiffness = 2.0
onset_stretch = 0.02
final_stretch = 0.05

MESH = pl.DeviceIdType.MESH
STRIPS = (0, -1, 1)
DIRECTIONS = tuple((es, et) for es in (-1, 1, 0) for et in (0, -1, 1) if (es, et) != (0, 0))
EDGE = 8


def whole_rows(per, es):
    return pl.ds(STRIPS.index(es) * per, per)


def edge_rows(per, es, et):
    return pl.ds(3 * per + (2 * STRIPS.index(es) + (et > 0)) * EDGE, EDGE)


def split_rows(rows):
    row = lax.broadcasted_iota(jnp.int32, rows.shape, 0)
    lead = jnp.where(row < 3, rows, jnp.where(row == 3, 1.0, 0.0))
    high = lead.astype(jnp.bfloat16).astype(jnp.float32)
    return jnp.concatenate([high, lead - high], axis=0).astype(jnp.bfloat16)


def pair_pull(first, second, bonds):
    def norm2(c):
        x, y, z = (second[c + i] - first(c + i) for i in range(3))
        return x * x + y * y + z * z

    now2, ref2 = norm2(0), norm2(3)
    inv_now, inv_ref = lax.rsqrt(now2), lax.rsqrt(ref2)
    ratio = now2 * inv_now * inv_ref
    influence = jnp.maximum(0.0, stiffness - ref2 * inv_ref * (stiffness / horizon))
    span = final_stretch - onset_stretch
    soften = jnp.clip((1.0 + final_stretch) / span - ratio * (1.0 / span), 0.0, 1.0)
    pull = (ratio - 1.0) * influence * (soften * inv_now)
    return jnp.where(bonds != 0, pull, 0.0)


def dot_rows(rows, matrix):
    return lax.dot_general(rows, matrix, (((1,), (0,)), ((), ())), preferred_element_type=jnp.float32)


def dot_columns(rows, matrix):
    return lax.dot_general(rows, matrix, (((1,), (1,)), ((), ())), preferred_element_type=jnp.float32)


def force_kernel(
    scalars_ref, ends_ref, coords_ref, displacement_ref, bonds_hbm, out_ref, received_ref,
    table, owned, spread, bonds, gains, forces, from_strip, from_edge,
    load_sem, send_sem, recv_sem, back_sem, home_sem,
):
    per, points = coords_ref.shape[1], coords_ref.shape[2]
    pair_count = bonds.shape[0]
    groups = load_sem.shape[0]
    group = pair_count // groups
    strip, tile = lax.axis_index("strip"), lax.axis_index("tile")
    strips, tiles = lax.axis_size("strip"), lax.axis_size("tile")

    def load(g):
        part = pl.ds(g * group, group)
        return pltpu.make_async_copy(bonds_hbm.at[part], bonds.at[part], load_sem.at[g])

    for g in range(groups):
        load(g).start()

    def exists(es, et):
        s, t = strip + es, tile + et
        return (s >= 0) & (s < strips) & (t >= 0) & (t < tiles)

    barrier = pltpu.get_barrier_semaphore()
    for es, et in DIRECTIONS:
        @pl.when(exists(es, et))
        def _(es=es, et=et):
            pl.semaphore_signal(
                barrier, inc=1, device_id=(strip + es, tile + et), device_id_type=MESH
            )

    place = lax.broadcasted_iota(jnp.int32, (per, points), 0) + tile * per
    for c in range(3):
        local = coords_ref[c]
        base = (4 * strip).astype(jnp.float32) if c == 0 else (
            4.0 * place.astype(jnp.float32) if c == 1 else 0.0)
        local = local - base - (3.5 if c == 2 else 1.5)
        now = local + displacement_ref[c]
        table[3 + c, 0:per, :] = local
        table[c, 0:per, :] = now
        owned[:, 3 + c, :] = local
        owned[:, c, :] = now
    for c in (6, 7):
        owned[:, c, :] = jnp.zeros((per, points), jnp.float32)

    near = sum(
        jnp.where(exists(es, et), 1, 0) for es, et in DIRECTIONS
    )
    pl.semaphore_wait(barrier, near)

    def halo(i):
        es, et = DIRECTIONS[i]
        if et == 0:
            source, target = pl.ds(0, per), whole_rows(per, -es)
        else:
            source = pl.ds(per - EDGE if et > 0 else 0, EDGE)
            target = edge_rows(per, -es, -et)
        return pltpu.make_async_remote_copy(
            src_ref=table.at[:, source],
            dst_ref=table.at[:, target],
            send_sem=send_sem.at[i],
            recv_sem=recv_sem.at[i],
            device_id=(strip + es, tile + et),
            device_id_type=MESH,
        )

    def back(i):
        es, et = DIRECTIONS[i]
        if et == 0:
            source, target = whole_rows(per, es), from_strip.at[0 if es < 0 else 1]
        else:
            source, target = edge_rows(per, es, et), from_edge.at[i]
        return pltpu.make_async_remote_copy(
            src_ref=forces.at[:, source],
            dst_ref=target,
            send_sem=back_sem.at[i],
            recv_sem=home_sem.at[i],
            device_id=(strip + es, tile + et),
            device_id_type=MESH,
        )

    def each(step, opposite):
        for i, (es, et) in enumerate(DIRECTIONS):
            here = exists(-es, -et) if opposite else exists(es, et)
            pl.when(here)(lambda i=i: step(i))

    each(lambda i: halo(i).start(), False)

    def widen(g, carry):
        columns = owned[pl.ds(g * (points // 8), points // 8)].reshape(points, points).T
        for j in range(points // 8):
            for c in range(6):
                column = columns[:, 8 * j + c : 8 * j + c + 1]
                spread[g * (points // 8) + j, c] = jnp.broadcast_to(column, (points, points))
        return carry

    lax.fori_loop(0, per * 8 // points, widen, 0)

    each(lambda i: halo(i).wait_recv(), True)

    chunk = math.gcd(points, 32)
    row = lax.broadcasted_iota(jnp.int32, (8, points), 0)

    def visit(k, carry):
        first, second = scalars_ref[0, k], scalars_ref[1, k]
        move_x = scalars_ref[2, k].astype(jnp.float32)
        move_y = scalars_ref[3, k].astype(jnp.float32)
        second_flat = [table[c, pl.ds(second, 1), :] for c in range(6)]
        moved = [
            second_flat[0] + move_x, second_flat[1] + move_y, second_flat[2],
            second_flat[3] + move_x, second_flat[4] + move_y, second_flat[5],
        ]
        leads, rests = [], []
        for at in range(0, points, chunk):
            pull = pair_pull(
                lambda c: spread[first, c, at : at + chunk, :], moved, bonds[k, at : at + chunk]
            )
            lead = pull.astype(jnp.bfloat16)
            leads.append(lead)
            rests.append((pull - lead.astype(jnp.float32)).astype(jnp.bfloat16))
        lead, rest = jnp.concatenate(leads, axis=0), jnp.concatenate(rests, axis=0)
        first_rows = owned[first]
        second_rows = jnp.where(
            row == 0, second_flat[0], jnp.where(row == 1, second_flat[1], second_flat[2])
        )
        first_split, second_split = split_rows(first_rows), split_rows(second_rows)
        to_first = dot_columns(second_split, lead) + dot_columns(second_split, rest)
        to_second = dot_rows(first_split, lead) + dot_rows(first_split, rest)
        to_first = to_first[:8] + to_first[8:]
        to_second = to_second[:8] + to_second[8:]
        move = jnp.where(row == 0, move_x, jnp.where(row == 1, move_y, 0.0))
        to_first = to_first - (first_rows - move) * to_first[3:4]
        to_second = to_second - (second_rows + move) * to_second[3:4]
        for c in range(3):
            gains[c, pl.ds(k, 1), :] = to_first[c : c + 1]
            gains[c, pl.ds(pair_count + k, 1), :] = to_second[c : c + 1]
        return carry

    def visit_group(g, carry):
        load(g).wait()
        return lax.fori_loop(0, group, lambda i, c: visit(g * group + i, c), carry, unroll=group)

    lax.fori_loop(0, groups, visit_group, 0)

    def pieces_of(start):
        pieces = []
        for c in range(3):
            value = gains[c, start : start + pair_count]
            for unused in range(3):
                piece = value.astype(jnp.bfloat16)
                pieces.append(piece)
                value = value - piece.astype(jnp.float32)
        return jnp.concatenate(pieces, axis=1)

    ends = ends_ref[...]
    second_pieces = pieces_of(pair_count)

    def gather(start, count, which, pieces):
        slot = lax.broadcasted_iota(jnp.int32, (count, pair_count), 0) + start
        weight = jnp.where(slot == ends[which : which + 1], 1.0, 0.0).astype(jnp.bfloat16)
        sums = dot_rows(weight, pieces)
        for c in range(3):
            parts = [sums[:, (3 * c + j) * points : (3 * c + j + 1) * points] for j in range(3)]
            yield parts[0] + (parts[1] + parts[2])

    for c, total in enumerate(gather(per, forces.shape[1] - per, 1, second_pieces)):
        forces[c, per:, :] = total
    each(lambda i: back(i).start(), False)
    both = zip(gather(0, per, 1, second_pieces), gather(0, per, 0, pieces_of(0)))
    for c, (second_total, first_total) in enumerate(both):
        forces[c, 0:per, :] = second_total + first_total

    def receive(i):
        es, et = DIRECTIONS[i]
        back(i).wait_recv()
        if et == 0:
            received_ref[...] += from_strip[0 if es < 0 else 1]
        else:
            at = per - EDGE if et < 0 else 0
            received_ref[:, at : at + EDGE, :] += from_edge[i]

    out_ref[...] = forces[:, 0:per, :]
    received_ref[...] = jnp.zeros_like(received_ref)
    each(receive, True)
    each(lambda i: halo(i).wait_send(), False)
    each(lambda i: back(i).wait_send(), False)


def on_device(coords, displacement, pairs, intact):
    per, points = coords.shape[0], coords.shape[2]
    pair_count = pairs.shape[0]
    groups = math.gcd(pair_count, 8)
    strip_tiles = per * lax.axis_size("tile")
    strip_index = lax.axis_index("strip")
    tile_index = lax.axis_index("tile")
    first, second = pairs.T[:1], pairs.T[1:]
    row = lax.broadcasted_iota(jnp.int32, (4, pair_count), 0)
    tiles = jnp.where(row == 0, first, second)
    beside = tiles // strip_tiles - strip_index
    order = jnp.where(beside == 0, 0, jnp.where(beside < 0, 1, 2))
    at = tiles % strip_tiles - tile_index * per
    edge = 3 * per + 2 * EDGE * order
    slot = jnp.where(at < 0, edge + EDGE - 1, jnp.where(at >= per, edge + EDGE, order * per + at))
    over = second // strip_tiles - first // strip_tiles
    along = second % strip_tiles - first % strip_tiles
    listed = jnp.where(row < 2, slot, 4 * jnp.where(row == 2, over, along))
    slots = 3 * per + 6 * EDGE
    many = len(DIRECTIONS)
    vmem = pl.BlockSpec(memory_space=pltpu.VMEM)
    own, received = pl.pallas_call(
        force_kernel,
        in_specs=[
            pl.BlockSpec(memory_space=pltpu.SMEM), vmem, vmem, vmem,
            pl.BlockSpec(memory_space=pl.ANY),
        ],
        out_specs=(vmem, vmem),
        out_shape=(jax.ShapeDtypeStruct((3, per, points), jnp.float32),) * 2,
        scratch_shapes=[
            pltpu.VMEM((6, slots, points), jnp.float32),
            pltpu.VMEM((per, 8, points), jnp.float32),
            pltpu.VMEM((per, 6, points, points), jnp.float32),
            pltpu.VMEM(intact.shape, jnp.int32),
            pltpu.VMEM((3, 2 * pair_count, points), jnp.float32),
            pltpu.VMEM((3, slots, points), jnp.float32),
            pltpu.VMEM((2, 3, per, points), jnp.float32),
            pltpu.VMEM((many, 3, EDGE, points), jnp.float32),
            pltpu.SemaphoreType.DMA((groups,)),
            pltpu.SemaphoreType.DMA((many,)),
            pltpu.SemaphoreType.DMA((many,)),
            pltpu.SemaphoreType.DMA((many,)),
            pltpu.SemaphoreType.DMA((many,)),
        ],
        compiler_params=pltpu.CompilerParams(collective_id=0, has_side_effects=True),
    )(listed, listed, coords.transpose(1, 0, 2), displacement.transpose(1, 0, 2), intact)
    return jnp.transpose(own + received, (1, 0, 2))


def solution(mesh):
    placed = (
        P(("strip", "tile"), None, None),
        P(("strip", "tile"), None, None),
        P(("strip", "tile"), None),
        P(("strip", "tile"), None, None),
    )
    return jax.shard_map(
        on_device,
        mesh=mesh,
        in_specs=placed,
        out_specs=P(("strip", "tile"), None, None),
        check_vma=False,
    )
```

profile of v0, /device:TPU:1, one launch (start us, length us, event | category | flops | bytes accessed | tf_op | source)
XLA Modules:
  0.0 27.3 jit_solution(12414423843488185450)
XLA Ops:
  0.0 0.8 %slice_bitcast_fusion.1 = (s32[64]{0:T(128)S(1)}, s32[64]{0:T(128)S(1)}, s32[64]{0:T(128)S(1)}, s32[64]{0:T(128)S(1)}) fusion(s32[2,64]{1,0:T(2,128)} %bitcast.15), kind=kLoop, calls=%fused_computation.26 | loop fusion | flops 1664 | bytes 1536 | tf_op jit(solution)/shard_map/jit(_where)/broadcast_in_dim | solution.py:256
  0.8 0.7 %multiply_select_fusion.scalars_ref.ends_ref = s32[4,64]{1,0:T(4,128)} fusion(s32[64]{0:T(128)S(1)} %get-tuple-element.11, s32[64]{0:T(128)S(1)} %get-tuple-element.10, s32[]{:T(128)S(6)} %axis_index.25, s32[]{:T(128)S(6)} %mul.18, s32[64]{0:T(128)S(1)} %get-tuple-element.12, s32[64]{0:T(128)S(1)} %get-tuple-element.9, ...), kind=kLoop, calls=%fused_computation.12 | loop fusion | flops 7936 | bytes 2068 | tf_op jit(solution)/shard_map/jit(_where)/select_n | solution.py:264
  1.5 24.3 %shard_map.46 = (f32[3,48,128]{2,1,0:T(8,128)}, f32[3,48,128]{2,1,0:T(8,128)}) custom-call(s32[4,64]{1,0:T(4,128)} %multiply_select_fusion.scalars_ref.ends_ref, s32[4,64]{1,0:T(4,128)} %multiply_select_fusion.scalars_ref.ends_ref, f32[3,48,128]{2,1,0:T(8,128)} %bitcast.13, f32[3,48,128]{2,1,0:T(8,128)} %bitcast.14, s32[64,128,128]{2,1,0:T(8,128)} %bonds_hbm.1), custom_call_target="tpu_custom_call" | custom-call | tf_op jit(solution)/shard_map/pallas_call | solution.py:268
  25.7 1.6 %add_bitcast_fusion = f32[48,3,128]{2,0,1:T(8,128)} fusion(f32[3,48,128]{2,1,0:T(8,128)} %get-tuple-element.7, f32[3,48,128]{2,1,0:T(8,128)} %get-tuple-element.8), kind=kLoop, calls=%fused_computation | loop fusion | flops 18432 | bytes 221184 | tf_op jit(solution)/shard_map/transpose | solution.py:293
  (2 shorter events, 0.0 us)
where the time goes:
time: 27.5 us; the launch traced here: 27.3 us
  Pallas kernels  24.3 us (88%)
  other arithmetic  3.02 us (11%)
    pallas_call x1, Pallas kernels, on_device(): pl.pallas_call(force_kernel, in_specs=[pl.BlockSpec(memory_space=pltpu.SM...  24.3 us
    transpose x1, other arithmetic, on_device(): return jnp.transpose(own + received, (1, 0, 2))  1.56 us
    broadcast_in_dim x1, other arithmetic, on_device(): tiles = jnp.where(row == 0, first, second)  0.77 us
    select_n x1, other arithmetic, on_device(): listed = jnp.where(row < 2, slot, 4 * jnp.where(row == 2, over, along))  0.67 us

commit v1 on v0

v1 whole, which is shorter than its diff:
```python
import math

import jax
import jax.numpy as jnp
from jax import lax
from jax.experimental import pallas as pl
from jax.experimental.pallas import tpu as pltpu
from jax.sharding import PartitionSpec as P

horizon = 3.0
stiffness = 2.0
onset_stretch = 0.02
final_stretch = 0.05
span = final_stretch - onset_stretch
scale = stiffness / (horizon * span)

MESH = pl.DeviceIdType.MESH
STRIPS = (0, -1, 1)
SIDES = (-1, 1)
EDGES = tuple((es, et) for es in STRIPS for et in SIDES)
BLOCK = 8
CENTRE = (1.5, 1.5, 3.5)
DIGITS = 4


def strip_rows(per, es):
    return pl.ds(STRIPS.index(es) * per, per)


def edge_of(es, et):
    return EDGES.index((es, et))


def dot_rows(rows, matrix):
    return lax.dot_general(rows, matrix, (((1,), (0,)), ((), ())), preferred_element_type=jnp.float32)


def dot_columns(rows, matrix):
    return lax.dot_general(rows, matrix, (((1,), (1,)), ((), ())), preferred_element_type=jnp.float32)


def pieces_of(value, count=3):
    pieces = []
    for unused in range(count):
        piece = value.astype(jnp.bfloat16)
        pieces.append(piece)
        value = value - piece.astype(jnp.float32)
    return pieces


def norm2(x, y, z):
    return x * x + y * y + z * z


def locate(a, b, strip, tile, strip_tiles, per):
    here = strip * strip_tiles
    place = a - here
    beside = b - here
    over = jnp.where(beside < 0, -1, jnp.where(beside >= strip_tiles, 1, 0))
    second_place = beside - over * strip_tiles
    at = second_place - tile * per
    order = jnp.where(over == 0, 0, jnp.where(over < 0, 1, 2))
    edge = 3 * per + 2 * order
    slot = jnp.where(at < 0, edge, jnp.where(at >= per, edge + 1, order * per + at))
    across = jnp.where(over == 0, 0, 1)
    sign = jnp.where(over == 0, second_place - place, over)
    first = jnp.clip(place - tile * per, 0, per - 1)
    return place, first, slot, across, sign


def force_kernel(
    pairs_hbm, coords_hbm, displacement_hbm, bonds_hbm, out_ref,
    pairs, ends_ref, coords, displacement, edge_out, edge_in, bonds, mask, owned, folded, halves,
    features, columns, wide_ref, wide_now, near, inverse, pulls, gains, back_strip, back_edge,
    from_strip, from_edge,
    in_sem, load_sem, halo_send, halo_recv, edge_send, edge_recv, back_send, back_recv,
    back_edge_send, back_edge_recv,
):
    per, points = coords_hbm.shape[1], coords_hbm.shape[2]
    pair_count = pairs_hbm.shape[1]
    slots = coords.shape[1]
    groups = load_sem.shape[0]
    group = pair_count // groups
    half = points // 2
    batches = per // BLOCK
    strip, tile = lax.axis_index("strip"), lax.axis_index("tile")
    strips, tiles = lax.axis_size("strip"), lax.axis_size("tile")
    strip_tiles = per * tiles

    own = pl.ds(0, per)
    inputs = [
        pltpu.make_async_copy(coords_hbm, coords.at[pl.ds(0, 3), own], in_sem.at[0]),
        pltpu.make_async_copy(displacement_hbm, displacement.at[pl.ds(0, 3), own], in_sem.at[1]),
        pltpu.make_async_copy(pairs_hbm, pairs, in_sem.at[2]),
        pltpu.make_async_copy(pairs_hbm, ends_ref, in_sem.at[3]),
    ]
    for copy in inputs:
        copy.start()

    def load(g):
        part = pl.ds(g * group, group)
        return pltpu.make_async_copy(bonds_hbm.at[part], bonds.at[part], load_sem.at[g])

    for g in range(groups):
        load(g).start()

    def exists(es, et):
        s, t = strip + es, tile + et
        return (s >= 0) & (s < strips) & (t >= 0) & (t < tiles)

    around = EDGES + tuple((es, 0) for es in SIDES)
    barrier = pltpu.get_barrier_semaphore()
    for es, et in around:
        @pl.when(exists(es, et))
        def _(es=es, et=et):
            pl.semaphore_signal(
                barrier, inc=1, device_id=(strip + es, tile + et), device_id_type=MESH
            )

    def remote(source, target, send, recv, es, et):
        return pltpu.make_async_remote_copy(
            src_ref=source, dst_ref=target, send_sem=send, recv_sem=recv,
            device_id=(strip + es, tile + et), device_id_type=MESH,
        )

    def halo(which, i):
        es = SIDES[i]
        table = (coords, displacement)[which]
        part = pl.ds(0, 3)
        return remote(
            table.at[part, own], table.at[part, strip_rows(per, -es)],
            halo_send.at[2 * which + i], halo_recv.at[2 * which + i], es, 0,
        )

    def edge(i):
        es, et = EDGES[i]
        return remote(
            edge_out.at[0 if et < 0 else 1], edge_in.at[edge_of(-es, -et)],
            edge_send.at[i], edge_recv.at[i], es, et,
        )

    def back(i):
        es = SIDES[i]
        return remote(back_strip.at[i], from_strip.at[i], back_send.at[i], back_recv.at[i], es, 0)

    def edge_back(i):
        es, et = EDGES[i]
        return remote(
            back_edge.at[i], from_edge.at[i], back_edge_send.at[i], back_edge_recv.at[i], es, et
        )

    def each_side(step, opposite):
        for i, es in enumerate(SIDES):
            pl.when(exists(-es if opposite else es, 0))(lambda i=i: step(i))

    def each_edge(step, opposite):
        for i, (es, et) in enumerate(EDGES):
            here = exists(-es, -et) if opposite else exists(es, et)
            pl.when(here)(lambda i=i: step(i))

    for copy in inputs:
        copy.wait()
    for i, at in enumerate((0, per - 1)):
        for c in range(3):
            edge_out[i, c : c + 1, :] = coords[c, at : at + 1, :]
            edge_out[i, 3 + c : 4 + c, :] = displacement[c, at : at + 1, :]

    pl.semaphore_wait(barrier, sum(jnp.where(exists(es, et), 1, 0) for es, et in around))
    each_edge(lambda i: edge(i).start(), False)
    each_side(lambda i: halo(0, i).start(), False)
    each_side(lambda i: halo(1, i).start(), False)

    row = lax.broadcasted_iota(jnp.int32, (BLOCK, points), 0)
    lane = lax.broadcasted_iota(jnp.int32, (BLOCK, points), 1)
    digits = (lax.rem(lane // DIGITS, DIGITS), lax.rem(lane, DIGITS))

    place = lax.broadcasted_iota(jnp.int32, (per, points), 0) + tile * per
    bases = (
        (DIGITS * strip).astype(jnp.float32) + CENTRE[0],
        (DIGITS * place).astype(jnp.float32) + CENTRE[1],
        CENTRE[2],
    )
    for c in range(3):
        local = coords[c, 0:per] - bases[c]
        owned[:, 4 + c, :] = local
        owned[:, c, :] = local + displacement[c, 0:per]
    owned[:, 3, :] = jnp.ones((per, points), jnp.float32)
    owned[:, 7, :] = jnp.zeros((per, points), jnp.float32)

    def order_of(source):
        odd, rest = source // half, lax.rem(source, half)
        block, i = rest // BLOCK, lax.rem(rest, BLOCK)
        quarter = half // 2
        high, wide = rest // quarter, lax.rem(rest, quarter) // BLOCK
        along = 2 * BLOCK * block + BLOCK * odd + i
        across = DIGITS * BLOCK * wide + DIGITS * i + 2 * odd + high
        return along, across

    to = lax.broadcasted_iota(jnp.int32, (points, points), 1)
    picks = [
        jnp.where(lax.broadcasted_iota(jnp.int32, (points, points), 0) == source, 1.0, 0.0).astype(jnp.bfloat16)
        for source in order_of(to)
    ]
    first_half = lax.broadcasted_iota(jnp.int32, (BLOCK * BLOCK, points), 1) < half

    def fold(g, carry):
        rows = owned[pl.ds(g * BLOCK, BLOCK)].reshape(BLOCK * BLOCK, points)
        pieces = pieces_of(rows)
        for across in range(2):
            parts = [dot_rows(piece, picks[across]) for piece in pieces]
            ordered = parts[0] + (parts[1] + parts[2])
            turned = pltpu.roll(ordered, half, 1)
            base = across * per + g * BLOCK
            folded[pl.ds(base, BLOCK)] = ordered.reshape(BLOCK, BLOCK, points)
            for h in range(2):
                twice = jnp.where(first_half, ordered, turned) if h == 0 else jnp.where(first_half, turned, ordered)
                high = twice.astype(jnp.bfloat16).astype(jnp.float32)
                both = jnp.concatenate(
                    [high.reshape(BLOCK, BLOCK, points), (twice - high).reshape(BLOCK, BLOCK, points)], axis=1
                )
                features[pl.ds((2 * across + h) * per + g * BLOCK, BLOCK)] = both.astype(jnp.bfloat16)
            flat = jnp.concatenate([ordered, turned], axis=0).T
            columns[across * batches + g] = flat[:half]
        return carry

    lax.fori_loop(0, batches, fold, 0)

    def scalars(k):
        return locate(pairs[0, k], pairs[1, k], strip, tile, strip_tiles, per)

    def lanes_of(across, sign):
        digit = jnp.where(jnp.full((BLOCK, points), across) == 1, digits[1], digits[0])
        moved = digit == jnp.where(sign > 0, DIGITS - 1, 0)
        step = jnp.where(across == 1, 1, DIGITS) * (DIGITS - 1)
        shift = jnp.where(sign > 0, step, points - step)
        return moved, shift

    def merge(value, moved, shift):
        return jnp.where(moved, pltpu.roll(value, shift, 1), value)

    def prepare(k, carry):
        unused, first, unused, across, sign = scalars(k)
        moved, shift = lanes_of(across, sign)
        main = jnp.where(sign > 0, 1, 0)
        which = across * batches + first // BLOCK
        index = jnp.where(moved, (1 - main) * half, main * half) + lax.rem(first, BLOCK) * BLOCK
        sources = [columns[which, j * BLOCK : (j + 1) * BLOCK, :] for j in range(half // BLOCK)]
        for c in range(3):
            for offset, target in ((4, wide_ref), (0, wide_now)):
                for j, source in enumerate(sources):
                    target[k, c, j * BLOCK : (j + 1) * BLOCK, :] = jnp.take_along_axis(
                        source, index + (offset + c), axis=1
                    )
        is_across = jnp.full((BLOCK, points), across) == 1
        is_odd = jnp.full((BLOCK, points), main) == 1
        quarter = half // 2 // BLOCK
        for j in range(half // BLOCK):
            high, wide = j // quarter, j % quarter
            along = [bonds[k, pl.ds((2 * j + odd) * BLOCK, BLOCK)] for odd in range(2)]
            strided = [
                bonds[k, pl.ds(DIGITS * BLOCK * wide + 2 * odd + high, BLOCK, stride=DIGITS)]
                for odd in range(2)
            ]
            even, odd = (jnp.where(is_across, strided[i], along[i]) for i in range(2))
            large, small = jnp.where(is_odd, odd, even), jnp.where(is_odd, even, odd)
            held = jnp.where(moved, pltpu.roll(small, shift, 1), large)
            mask[k, j * BLOCK : (j + 1) * BLOCK] = jnp.where(held != 0, scale, 0.0)
        return carry

    def by_group(step, before):
        def run(g, carry):
            before(g)
            return lax.fori_loop(0, group, lambda i, c: step(g * group + i, c), carry, unroll=group)

        lax.fori_loop(0, groups, run, 0)

    by_group(prepare, lambda g: load(g).wait())

    def unpack_edges(which):
        table = (coords, displacement)[which]
        for i, (es, et) in enumerate(EDGES):
            @pl.when(exists(es, et))
            def _(i=i):
                for c in range(3):
                    at = 3 * per + i
                    table[c, at : at + 1, :] = edge_in[i, 3 * which + c : 3 * which + c + 1, :]

    each_edge(lambda i: edge(i).wait_recv(), True)
    unpack_edges(0)
    unpack_edges(1)
    each_side(lambda i: halo(0, i).wait_recv(), True)

    flat_coords = coords.reshape(coords.shape[0] * slots, points)
    flat_displacement = displacement.reshape(displacement.shape[0] * slots, points)
    chunk = half // 2

    def second_rows(place, slot):
        rows = flat_coords[pl.ds(slot, BLOCK, stride=slots), :]
        by = (DIGITS * place).astype(jnp.float32) + CENTRE[1]
        return rows - jnp.where(row == 0, bases[0], jnp.where(row == 1, by, bases[2]))

    def spread(rows, c):
        return jnp.broadcast_to(rows[c : c + 1], (chunk, points))

    def refer(k, carry):
        place, unused, slot, across, sign = scalars(k)
        moved, shift = lanes_of(across, sign)
        rows = merge(second_rows(place, slot), moved, shift)
        for at in range(0, half, chunk):
            part = pl.ds(at, chunk)
            ref2 = norm2(*(spread(rows, c) - wide_ref[k, c, part, :] for c in range(3)))
            inv_ref = lax.rsqrt(ref2)
            inverse[k, part] = inv_ref
            near[k, part] = jnp.maximum(0.0, horizon - ref2 * inv_ref) * mask[k, part]
        return carry

    by_group(refer, lambda g: None)

    each_side(lambda i: halo(1, i).wait_recv(), True)

    def second_now(place, slot, moved, shift):
        rows = second_rows(place, slot) + flat_displacement[pl.ds(slot, BLOCK, stride=slots), :]
        rows = jnp.where(row < 3, rows, jnp.where(row == 3, 1.0, 0.0))
        return merge(rows, moved, shift)

    def act(k, carry):
        place, first, slot, across, sign = scalars(k)
        moved, shift = lanes_of(across, sign)
        main = jnp.where(sign > 0, 1, 0)
        rows = second_now(place, slot, moved, shift)
        leads, rests = [], []
        for at in range(0, half, chunk):
            part = pl.ds(at, chunk)
            now2 = norm2(*(spread(rows, c) - wide_now[k, c, part, :] for c in range(3)))
            inv_now, inv_ref = lax.rsqrt(now2), inverse[k, part]
            soften = jnp.clip((1.0 + final_stretch) - now2 * inv_now * inv_ref, 0.0, span)
            pull = (inv_ref - inv_now) * near[k, part] * soften
            lead = pull.astype(jnp.bfloat16)
            leads.append(lead)
            rests.append((pull - lead.astype(jnp.float32)).astype(jnp.bfloat16))
        pull = jnp.concatenate(leads + rests, axis=0)
        pulls[k] = pull
        at = 2 * across * per + first
        both = jnp.concatenate([features[at + main * per], features[at + (1 - main) * per]], axis=0)
        sums = dot_rows(both, pull)
        sums = [sums[i * BLOCK : (i + 1) * BLOCK] for i in range(4)]
        gain = jnp.where(moved, sums[2] + sums[3], sums[0] + sums[1])
        gain = gain - rows * gain[3:4]
        gain = jnp.where(moved, 0.0, gain) + pltpu.roll(jnp.where(moved, gain, 0.0), points - shift, 1)
        for c in range(3):
            gains[c, pl.ds(k, 1), :] = gain[c : c + 1]
        return carry

    by_group(act, lambda g: None)

    ends = ends_ref[...]
    unused, first_ends, second_ends, across_ends, unused = locate(
        ends[0:1], ends[1:2], strip, tile, strip_tiles, per
    )

    def row_pieces():
        pieces = []
        for c in range(3):
            pieces += pieces_of(gains[c])
        return jnp.concatenate(pieces, axis=1)

    def gather(start, count, listed, pieces):
        slot = lax.broadcasted_iota(jnp.int32, (count, pair_count), 0) + start
        weight = jnp.where(slot == listed, 1.0, 0.0).astype(jnp.bfloat16)
        sums = dot_rows(weight, pieces)
        totals = []
        for c in range(3):
            parts = [sums[:, (3 * c + j) * points : (3 * c + j + 1) * points] for j in range(3)]
            totals.append(parts[0] + (parts[1] + parts[2]))
        return totals

    second_pieces = row_pieces()
    for c, total in enumerate(gather(3 * per, BLOCK, second_ends, second_pieces)):
        for i in range(len(EDGES)):
            back_edge[i, c : c + 1, :] = total[i : i + 1]
    each_edge(lambda i: edge_back(i).start(), False)
    for i, es in enumerate(SIDES):
        for c, total in enumerate(gather(STRIPS.index(es) * per, per, second_ends, second_pieces)):
            back_strip[i, c] = total
    each_side(lambda i: back(i).start(), False)
    for c, total in enumerate(gather(0, per, second_ends, second_pieces)):
        out_ref[c] = total

    def react(k, carry):
        place, first, slot, across, sign = scalars(k)
        moved, shift = lanes_of(across, sign)
        main = jnp.where(sign > 0, 1, 0)
        rows = second_now(place, slot, moved, shift)
        sides = []
        for side in (jnp.where(moved, 0.0, rows), jnp.where(moved, rows, 0.0)):
            high = side.astype(jnp.bfloat16).astype(jnp.float32)
            sides += [high, side - high]
        sums = dot_columns(jnp.concatenate(sides, axis=0).astype(jnp.bfloat16), pulls[k])
        sums = [sums[i * BLOCK : (i + 1) * BLOCK] for i in range(4)]
        large, small = (value + pltpu.roll(value, half, 1) for value in (sums[0] + sums[1], sums[2] + sums[3]))
        odd = jnp.where(lane < half, 0, 1)
        gain = jnp.where(odd == main, large, small)
        gain = gain - folded[across * per + first] * gain[3:4]
        for c in range(3):
            gains[c, pl.ds(k, 1), :] = gain[c : c + 1]
        return carry

    by_group(react, lambda g: None)

    first_pieces = row_pieces()
    sums = [
        gather(0, per, jnp.where(across_ends == across, first_ends, -1), first_pieces) for across in range(2)
    ]
    unfold = jnp.concatenate(picks, axis=1)
    for c in range(3):
        both = jnp.concatenate([sums[0][c], sums[1][c]], axis=1)
        parts = [dot_columns(piece, unfold) for piece in pieces_of(both)]
        out_ref[c] += parts[0] + (parts[1] + parts[2])

    def receive_edge(i):
        es, et = EDGES[i]
        edge_back(i).wait_recv()
        at = per - 1 if et < 0 else 0
        for c in range(3):
            out_ref[c, at : at + 1, :] += from_edge[i, c : c + 1, :]

    def receive(i):
        back(i).wait_recv()
        out_ref[...] += from_strip[i]

    each_edge(receive_edge, True)
    each_side(receive, True)
    for which in range(2):
        each_side(lambda i: halo(which, i).wait_send(), False)
    each_edge(lambda i: edge(i).wait_send(), False)
    each_edge(lambda i: edge_back(i).wait_send(), False)
    each_side(lambda i: back(i).wait_send(), False)


def on_device(coords, displacement, pairs, intact):
    per, points = coords.shape[0], coords.shape[2]
    pair_count = pairs.shape[0]
    groups = math.gcd(pair_count, 8)
    slots = 3 * per + BLOCK
    half = points // 2
    batches = per // BLOCK
    f32 = jnp.float32
    hbm = pl.BlockSpec(memory_space=pltpu.HBM)
    total = pl.pallas_call(
        force_kernel,
        in_specs=[hbm] * 4,
        out_specs=pl.BlockSpec(memory_space=pltpu.VMEM),
        out_shape=jax.ShapeDtypeStruct((3, per, points), f32),
        scratch_shapes=[
            pltpu.SMEM((2, pair_count), jnp.int32),
            pltpu.VMEM((2, pair_count), jnp.int32),
            pltpu.VMEM((BLOCK, slots, points), f32),
            pltpu.VMEM((BLOCK, slots, points), f32),
            pltpu.VMEM((2, BLOCK, points), f32),
            pltpu.VMEM((len(EDGES), BLOCK, points), f32),
            pltpu.VMEM(intact.shape, jnp.int32),
            pltpu.VMEM((pair_count, half, points), f32),
            pltpu.VMEM((per, BLOCK, points), f32),
            pltpu.VMEM((2 * per, BLOCK, points), f32),
            pltpu.VMEM((BLOCK, points), f32),
            pltpu.VMEM((4 * per, 2 * BLOCK, points), jnp.bfloat16),
            pltpu.VMEM((2 * batches, half, points), f32),
            pltpu.VMEM((pair_count, 3, half, points), f32),
            pltpu.VMEM((pair_count, 3, half, points), f32),
            pltpu.VMEM((pair_count, half, points), f32),
            pltpu.VMEM((pair_count, half, points), f32),
            pltpu.VMEM((pair_count, points, points), jnp.bfloat16),
            pltpu.VMEM((3, pair_count, points), f32),
            pltpu.VMEM((2, 3, per, points), f32),
            pltpu.VMEM((len(EDGES), BLOCK, points), f32),
            pltpu.VMEM((2, 3, per, points), f32),
            pltpu.VMEM((len(EDGES), BLOCK, points), f32),
            pltpu.SemaphoreType.DMA((4,)),
            pltpu.SemaphoreType.DMA((groups,)),
            pltpu.SemaphoreType.DMA((4,)),
            pltpu.SemaphoreType.DMA((4,)),
            pltpu.SemaphoreType.DMA((len(EDGES),)),
            pltpu.SemaphoreType.DMA((len(EDGES),)),
            pltpu.SemaphoreType.DMA((2,)),
            pltpu.SemaphoreType.DMA((2,)),
            pltpu.SemaphoreType.DMA((len(EDGES),)),
            pltpu.SemaphoreType.DMA((len(EDGES),)),
        ],
        compiler_params=pltpu.CompilerParams(
            collective_id=0, has_side_effects=True, vmem_limit_bytes=60 * 1024 * 2**10
        ),
    )(pairs.T, coords.transpose(1, 0, 2), displacement.transpose(1, 0, 2), intact)
    return jnp.transpose(total, (1, 0, 2))


def solution(mesh):
    placed = (
        P(("strip", "tile"), None, None),
        P(("strip", "tile"), None, None),
        P(("strip", "tile"), None),
        P(("strip", "tile"), None, None),
    )
    return jax.shard_map(
        on_device,
        mesh=mesh,
        in_specs=placed,
        out_specs=P(("strip", "tile"), None, None),
        check_vma=False,
    )
```

time: 27.5 us -> 24.4 us (0.89)
  the two profiles are of different devices: /device:TPU:1 before, /device:TPU:0 now
where the time goes in v1:
time: 24.4 us; the launch traced here: 24.2 us
  Pallas kernels  22.7 us (93%)
  local copies, waits for them, and re-layouts  1.52 us (6%)
    pallas_call x1, Pallas kernels, on_device(): pl.pallas_call(force_kernel, in_specs=[hbm] * 4, out_specs=pl.BlockSpec(m...  22.7 us
    unnamed x1, local copies, waits for them, and re-layouts  1.52 us

profile of v1, /device:TPU:0, one launch (start us, length us, event | category | flops | bytes accessed | tf_op | source)
XLA Modules:
  0.0 24.2 jit_solution(10188676784703722872)
XLA Ops:
  0.0 22.7 %shard_map.46 = f32[3,48,128]{2,1,0:T(8,128)} custom-call(s32[2,64]{1,0:T(2,128)} %bitcast.7, f32[3,48,128]{2,1,0:T(8,128)} %bitcast.5, f32[3,48,128]{2,1,0:T(8,128)} %bitcast.6, s32[64,128,128]{2,1,0:T(8,128)} %bonds_hbm.1), custom_call_target="tpu_custom_call" | custom-call | tf_op jit(solution)/shard_map/pallas_call | solution.py:449
  22.7 1.5 %copy.6 = f32[48,3,128]{2,0,1:T(8,128)} copy(f32[48,3,128]{2,0,1:T(8,128)} %bitcast.4) | data formatting | bytes 147456

commit v2 on v1

--- a/solution.py
+++ b/solution.py
@@ -63,17 +63,17 @@
     edge = 3 * per + 2 * order
     slot = jnp.where(at < 0, edge, jnp.where(at >= per, edge + 1, order * per + at))
     across = jnp.where(over == 0, 0, 1)
-    sign = jnp.where(over == 0, second_place - place, over)
+    main = jnp.where(jnp.where(over == 0, second_place - place, over) > 0, 1, 0)
     first = jnp.clip(place - tile * per, 0, per - 1)
-    return place, first, slot, across, sign
+    return place, first, slot, across, main
 
 
 def force_kernel(
     pairs_hbm, coords_hbm, displacement_hbm, bonds_hbm, out_ref,
-    pairs, ends_ref, coords, displacement, edge_out, edge_in, bonds, mask, owned, folded, halves,
-    features, columns, wide_ref, wide_now, near, inverse, pulls, gains, back_strip, back_edge,
+    listed, plan, ends_ref, lanes, coords, displacement, edge_out, edge_in, bonds, mask, owned, folded,
+    features, columns, wide_ref, wide_now, rows_ref, near, inverse, pulls, gains, back_strip, back_edge,
     from_strip, from_edge,
-    in_sem, load_sem, halo_send, halo_recv, edge_send, edge_recv, back_send, back_recv,
+    in_sem, plan_sem, load_sem, halo_send, halo_recv, edge_send, edge_recv, back_send, back_recv,
     back_edge_send, back_edge_recv,
 ):
     per, points = coords_hbm.shape[1], coords_hbm.shape[2]
@@ -89,10 +89,9 @@
 
     own = pl.ds(0, per)
     inputs = [
+        pltpu.make_async_copy(pairs_hbm, ends_ref, in_sem.at[2]),
         pltpu.make_async_copy(coords_hbm, coords.at[pl.ds(0, 3), own], in_sem.at[0]),
         pltpu.make_async_copy(displacement_hbm, displacement.at[pl.ds(0, 3), own], in_sem.at[1]),
-        pltpu.make_async_copy(pairs_hbm, pairs, in_sem.at[2]),
-        pltpu.make_async_copy(pairs_hbm, ends_ref, in_sem.at[3]),
     ]
     for copy in inputs:
         copy.start()
@@ -158,26 +157,39 @@
             here = exists(-es, -et) if opposite else exists(es, et)
             pl.when(here)(lambda i=i: step(i))
 
-    for copy in inputs:
-        copy.wait()
-    for i, at in enumerate((0, per - 1)):
-        for c in range(3):
-            edge_out[i, c : c + 1, :] = coords[c, at : at + 1, :]
-            edge_out[i, 3 + c : 4 + c, :] = displacement[c, at : at + 1, :]
-
-    pl.semaphore_wait(barrier, sum(jnp.where(exists(es, et), 1, 0) for es, et in around))
-    each_edge(lambda i: edge(i).start(), False)
-    each_side(lambda i: halo(0, i).start(), False)
-    each_side(lambda i: halo(1, i).start(), False)
-
     row = lax.broadcasted_iota(jnp.int32, (BLOCK, points), 0)
     lane = lax.broadcasted_iota(jnp.int32, (BLOCK, points), 1)
     digits = (lax.rem(lane // DIGITS, DIGITS), lax.rem(lane, DIGITS))
-
-    place = lax.broadcasted_iota(jnp.int32, (per, points), 0) + tile * per
+    for across in range(2):
+        for main in range(2):
+            moved = digits[across] == (DIGITS - 1) * main
+            lanes[2 * across + main] = jnp.where(moved, 1 - main, main) * half
+
+    inputs[0].wait()
+    ends = ends_ref[...]
+    place, first, slot, across, main = locate(ends[0:1], ends[1:2], strip, tile, strip_tiles, per)
+    step = jnp.where(across == 1, 1, DIGITS) * (DIGITS - 1)
+    entries = (
+        slot, place, across * batches + first // BLOCK, lax.rem(first, BLOCK) * BLOCK,
+        jnp.where(main == 1, step, points - step), 2 * across + main,
+        (2 * across + main) * per + first, (2 * across + 1 - main) * per + first,
+        across * per + first,
+    )
+    for i, entry in enumerate(entries):
+        listed[i : i + 1, :] = entry
+    first_ends, second_ends, across_ends = first, slot, across
+
+    for copy in inputs[1:]:
+        copy.wait()
+    for i, at in enumerate((0, per - 1)):
+        for c in range(3):
+            edge_out[i, c : c + 1, :] = coords[c, at : at + 1, :]
+            edge_out[i, 3 + c : 4 + c, :] = displacement[c, at : at + 1, :]
+
+    places = lax.broadcasted_iota(jnp.int32, (per, points), 0) + tile * per
     bases = (
         (DIGITS * strip).astype(jnp.float32) + CENTRE[0],
-        (DIGITS * place).astype(jnp.float32) + CENTRE[1],
+        (DIGITS * places).astype(jnp.float32) + CENTRE[1],
         CENTRE[2],
     )
     for c in range(3):
@@ -223,38 +235,41 @@
             columns[across * batches + g] = flat[:half]
         return carry
 
-    lax.fori_loop(0, batches, fold, 0)
-
-    def scalars(k):
-        return locate(pairs[0, k], pairs[1, k], strip, tile, strip_tiles, per)
-
-    def lanes_of(across, sign):
-        digit = jnp.where(jnp.full((BLOCK, points), across) == 1, digits[1], digits[0])
-        moved = digit == jnp.where(sign > 0, DIGITS - 1, 0)
-        step = jnp.where(across == 1, 1, DIGITS) * (DIGITS - 1)
-        shift = jnp.where(sign > 0, step, points - step)
-        return moved, shift
+    planned = pltpu.make_async_copy(listed, plan, plan_sem)
+    planned.start()
+    lax.fori_loop(0, batches, fold, 0, unroll=batches)
+
+    pl.semaphore_wait(barrier, sum(jnp.where(exists(es, et), 1, 0) for es, et in around))
+    each_edge(lambda i: edge(i).start(), False)
+    each_side(lambda i: halo(0, i).start(), False)
+    each_side(lambda i: halo(1, i).start(), False)
+    planned.wait()
 
     def merge(value, moved, shift):
         return jnp.where(moved, pltpu.roll(value, shift, 1), value)
 
+    def moved_of(kind):
+        main = lax.rem(kind, 2)
+        return lanes[kind] != jnp.full((BLOCK, points), main * half)
+
+    pieces_count = half // BLOCK
+
     def prepare(k, carry):
-        unused, first, unused, across, sign = scalars(k)
-        moved, shift = lanes_of(across, sign)
-        main = jnp.where(sign > 0, 1, 0)
-        which = across * batches + first // BLOCK
-        index = jnp.where(moved, (1 - main) * half, main * half) + lax.rem(first, BLOCK) * BLOCK
-        sources = [columns[which, j * BLOCK : (j + 1) * BLOCK, :] for j in range(half // BLOCK)]
+        which, base, kind, shift = plan[2, k], plan[3, k], plan[5, k], plan[4, k]
+        index = lanes[kind] + base
+        sources = [columns[which, j * BLOCK : (j + 1) * BLOCK, :] for j in range(pieces_count)]
         for c in range(3):
             for offset, target in ((4, wide_ref), (0, wide_now)):
                 for j, source in enumerate(sources):
                     target[k, c, j * BLOCK : (j + 1) * BLOCK, :] = jnp.take_along_axis(
                         source, index + (offset + c), axis=1
                     )
-        is_across = jnp.full((BLOCK, points), across) == 1
-        is_odd = jnp.full((BLOCK, points), main) == 1
-        quarter = half // 2 // BLOCK
-        for j in range(half // BLOCK):
+        moved = moved_of(kind)
+        is_across = jnp.full((BLOCK, points), kind // 2) == 1
+        is_odd = jnp.full((BLOCK, points), lax.rem(kind, 2)) == 1
+        quarter = pieces_count // 2
+        larges, packed = [], 0
+        for j in range(pieces_count):
             high, wide = j // quarter, j % quarter
             along = [bonds[k, pl.ds((2 * j + odd) * BLOCK, BLOCK)] for odd in range(2)]
             strided = [
@@ -262,19 +277,23 @@
                 for odd in range(2)
             ]
             even, odd = (jnp.where(is_across, strided[i], along[i]) for i in range(2))
-            large, small = jnp.where(is_odd, odd, even), jnp.where(is_odd, even, odd)
-            held = jnp.where(moved, pltpu.roll(small, shift, 1), large)
+            larges.append(jnp.where(is_odd, odd, even))
+            packed = packed + jnp.where(is_odd, even, odd) * (1 << j)
+        packed = pltpu.roll(packed, shift, 1)
+        for j, large in enumerate(larges):
+            held = jnp.where(moved, packed & (1 << j), large)
             mask[k, j * BLOCK : (j + 1) * BLOCK] = jnp.where(held != 0, scale, 0.0)
         return carry
 
-    def by_group(step, before):
+    def by_group(step, size):
         def run(g, carry):
-            before(g)
-            return lax.fori_loop(0, group, lambda i, c: step(g * group + i, c), carry, unroll=group)
-
-        lax.fori_loop(0, groups, run, 0)
-
-    by_group(prepare, lambda g: load(g).wait())
+            return lax.fori_loop(0, size, lambda i, c: step(g * size + i, c), carry, unroll=size)
+
+        lax.fori_loop(0, pair_count // size, run, 0)
+
+    for g in range(groups):
+        load(g).wait()
+    by_group(prepare, math.gcd(pair_count, 8))
 
     def unpack_edges(which):
         table = (coords, displacement)[which]
@@ -294,18 +313,17 @@
     flat_displacement = displacement.reshape(displacement.shape[0] * slots, points)
     chunk = half // 2
 
-    def second_rows(place, slot):
-        rows = flat_coords[pl.ds(slot, BLOCK, stride=slots), :]
-        by = (DIGITS * place).astype(jnp.float32) + CENTRE[1]
-        return rows - jnp.where(row == 0, bases[0], jnp.where(row == 1, by, bases[2]))
-
     def spread(rows, c):
         return jnp.broadcast_to(rows[c : c + 1], (chunk, points))
 
     def refer(k, carry):
-        place, unused, slot, across, sign = scalars(k)
-        moved, shift = lanes_of(across, sign)
-        rows = merge(second_rows(place, slot), moved, shift)
+        slot, place, kind, shift = plan[0, k], plan[1, k], plan[5, k], plan[4, k]
+        moved = moved_of(kind)
+        by = (DIGITS * place).astype(jnp.float32) + CENTRE[1]
+        rows = flat_coords[pl.ds(slot, BLOCK, stride=slots), :]
+        rows = rows - jnp.where(row == 0, bases[0], jnp.where(row == 1, by, bases[2]))
+        rows = merge(jnp.where(row < 3, rows, jnp.where(row == 3, 1.0, 0.0)), moved, shift)
+        rows_ref[k] = rows
         for at in range(0, half, chunk):
             part = pl.ds(at, chunk)
             ref2 = norm2(*(spread(rows, c) - wide_ref[k, c, part, :] for c in range(3)))
@@ -314,20 +332,16 @@
             near[k, part] = jnp.maximum(0.0, horizon - ref2 * inv_ref) * mask[k, part]
         return carry
 
-    by_group(refer, lambda g: None)
+    by_group(refer, math.gcd(pair_count, 16))
 
     each_side(lambda i: halo(1, i).wait_recv(), True)
 
-    def second_now(place, slot, moved, shift):
-        rows = second_rows(place, slot) + flat_displacement[pl.ds(slot, BLOCK, stride=slots), :]
-        rows = jnp.where(row < 3, rows, jnp.where(row == 3, 1.0, 0.0))
-        return merge(rows, moved, shift)
-
     def act(k, carry):
-        place, first, slot, across, sign = scalars(k)
-        moved, shift = lanes_of(across, sign)
-        main = jnp.where(sign > 0, 1, 0)
-        rows = second_now(place, slot, moved, shift)
+        slot, kind, shift = plan[0, k], plan[5, k], plan[4, k]
+        moved = moved_of(kind)
+        shifts = jnp.where(row < 3, flat_displacement[pl.ds(slot, BLOCK, stride=slots), :], 0.0)
+        rows = rows_ref[k] + merge(shifts, moved, shift)
+        rows_ref[k] = rows
         leads, rests = [], []
         for at in range(0, half, chunk):
             part = pl.ds(at, chunk)
@@ -340,8 +354,7 @@
             rests.append((pull - lead.astype(jnp.float32)).astype(jnp.bfloat16))
         pull = jnp.concatenate(leads + rests, axis=0)
         pulls[k] = pull
-        at = 2 * across * per + first
-        both = jnp.concatenate([features[at + main * per], features[at + (1 - main) * per]], axis=0)
+        both = jnp.concatenate([features[plan[6, k]], features[plan[7, k]]], axis=0)
         sums = dot_rows(both, pull)
         sums = [sums[i * BLOCK : (i + 1) * BLOCK] for i in range(4)]
         gain = jnp.where(moved, sums[2] + sums[3], sums[0] + sums[1])
@@ -351,12 +364,7 @@
             gains[c, pl.ds(k, 1), :] = gain[c : c + 1]
         return carry
 
-    by_group(act, lambda g: None)
-
-    ends = ends_ref[...]
-    unused, first_ends, second_ends, across_ends, unused = locate(
-        ends[0:1], ends[1:2], strip, tile, strip_tiles, per
-    )
+    by_group(act, math.gcd(pair_count, 32))
 
     def row_pieces():
         pieces = []
@@ -387,10 +395,9 @@
         out_ref[c] = total
 
     def react(k, carry):
-        place, first, slot, across, sign = scalars(k)
-        moved, shift = lanes_of(across, sign)
-        main = jnp.where(sign > 0, 1, 0)
-        rows = second_now(place, slot, moved, shift)
+        kind = plan[5, k]
+        moved = moved_of(kind)
+        rows = rows_ref[k]
         sides = []
         for side in (jnp.where(moved, 0.0, rows), jnp.where(moved, rows, 0.0)):
             high = side.astype(jnp.bfloat16).astype(jnp.float32)
@@ -399,13 +406,13 @@
         sums = [sums[i * BLOCK : (i + 1) * BLOCK] for i in range(4)]
         large, small = (value + pltpu.roll(value, half, 1) for value in (sums[0] + sums[1], sums[2] + sums[3]))
         odd = jnp.where(lane < half, 0, 1)
-        gain = jnp.where(odd == main, large, small)
-        gain = gain - folded[across * per + first] * gain[3:4]
+        gain = jnp.where(odd == jnp.full((BLOCK, points), lax.rem(kind, 2)), large, small)
+        gain = gain - folded[plan[8, k]] * gain[3:4]
         for c in range(3):
             gains[c, pl.ds(k, 1), :] = gain[c : c + 1]
         return carry
 
-    by_group(react, lambda g: None)
+    by_group(react, math.gcd(pair_count, 16))
 
     first_pieces = row_pieces()
     sums = [
@@ -450,10 +457,12 @@
         force_kernel,
         in_specs=[hbm] * 4,
         out_specs=pl.BlockSpec(memory_space=pltpu.VMEM),
-        out_shape=jax.ShapeDtypeStruct((3, per, points), f32),
+        out_shape=pltpu.VMEM((3, per, points), f32),
         scratch_shapes=[
-            pltpu.SMEM((2, pair_count), jnp.int32),
+            pltpu.VMEM((2 * BLOCK, pair_count), jnp.int32),
+            pltpu.SMEM((2 * BLOCK, pair_count), jnp.int32),
             pltpu.VMEM((2, pair_count), jnp.int32),
+            pltpu.VMEM((4, BLOCK, points), jnp.int32),
             pltpu.VMEM((BLOCK, slots, points), f32),
             pltpu.VMEM((BLOCK, slots, points), f32),
             pltpu.VMEM((2, BLOCK, points), f32),
@@ -462,11 +471,11 @@
             pltpu.VMEM((pair_count, half, points), f32),
             pltpu.VMEM((per, BLOCK, points), f32),
             pltpu.VMEM((2 * per, BLOCK, points), f32),
-            pltpu.VMEM((BLOCK, points), f32),
             pltpu.VMEM((4 * per, 2 * BLOCK, points), jnp.bfloat16),
             pltpu.VMEM((2 * batches, half, points), f32),
             pltpu.VMEM((pair_count, 3, half, points), f32),
             pltpu.VMEM((pair_count, 3, half, points), f32),
+            pltpu.VMEM((pair_count, BLOCK, points), f32),
             pltpu.VMEM((pair_count, half, points), f32),
             pltpu.VMEM((pair_count, half, points), f32),
             pltpu.VMEM((pair_count, points, points), jnp.bfloat16),
@@ -475,7 +484,8 @@
             pltpu.VMEM((len(EDGES), BLOCK, points), f32),
             pltpu.VMEM((2, 3, per, points), f32),
             pltpu.VMEM((len(EDGES), BLOCK, points), f32),
-            pltpu.SemaphoreType.DMA((4,)),
+            pltpu.SemaphoreType.DMA((3,)),
+            pltpu.SemaphoreType.DMA,
             pltpu.SemaphoreType.DMA((groups,)),
             pltpu.SemaphoreType.DMA((4,)),
             pltpu.SemaphoreType.DMA((4,)),

time: 24.4 us -> 18.2 us (0.75)
  Pallas kernels: 22.7 us -> 17.4 us
  local copies, waits for them, and re-layouts: 1.52 us -> 0.64 us
    pallas_call x1, Pallas kernels: 22.7 us -> 17.4 us  [on_device(): pl.pallas_call(force_kernel, in_specs=[hbm] * 4, out_specs=pl.BlockSpec(m...]
    unnamed x1, local copies, waits for them, and re-layouts: 1.52 us -> 0.64 us
where the time goes in v2:
time: 18.2 us; the launch traced here: 18.1 us
  Pallas kernels  17.4 us (96%)
  local copies, waits for them, and re-layouts  0.64 us (4%)
    pallas_call x1, Pallas kernels, on_device(): pl.pallas_call(force_kernel, in_specs=[hbm] * 4, out_specs=pl.BlockSpec(m...  17.4 us
    unnamed x1, local copies, waits for them, and re-layouts  0.64 us

profile of v2, /device:TPU:0, one launch (start us, length us, event | category | flops | bytes accessed | tf_op | source)
XLA Modules:
  0.0 18.1 jit_solution(2736315951069777285)
XLA Ops:
  0.0 17.4 %shard_map.46 = f32[3,48,128]{2,1,0:T(8,128)S(1)} custom-call(s32[2,64]{1,0:T(2,128)} %bitcast.7, f32[3,48,128]{2,1,0:T(8,128)} %bitcast.5, f32[3,48,128]{2,1,0:T(8,128)} %bitcast.6, s32[64,128,128]{2,1,0:T(8,128)} %bonds_hbm.1), custom_call_target="tpu_custom_call" | custom-call | tf_op jit(solution)/shard_map/pallas_call | solution.py:456
  17.4 0.6 %copy.6 = f32[48,3,128]{2,0,1:T(8,128)} copy(f32[48,3,128]{2,0,1:T(8,128)S(1)} %bitcast.4) | data formatting | bytes 147456

commit v3 on v2

--- a/solution.py
+++ b/solution.py
@@ -12,15 +12,19 @@
 onset_stretch = 0.02
 final_stretch = 0.05
 span = final_stretch - onset_stretch
-scale = stiffness / (horizon * span)
+scale = stiffness / horizon
 
 MESH = pl.DeviceIdType.MESH
 STRIPS = (0, -1, 1)
 SIDES = (-1, 1)
 EDGES = tuple((es, et) for es in STRIPS for et in SIDES)
+AROUND = EDGES[2:] + tuple((es, 0) for es in SIDES) + EDGES[:2]
 BLOCK = 8
 CENTRE = (1.5, 1.5, 3.5)
 DIGITS = 4
+PIECES = 2
+AHEAD = 2
+STEP = 8
 
 
 def strip_rows(per, es):
@@ -39,7 +43,7 @@
     return lax.dot_general(rows, matrix, (((1,), (1,)), ((), ())), preferred_element_type=jnp.float32)
 
 
-def pieces_of(value, count=3):
+def pieces_of(value, count):
     pieces = []
     for unused in range(count):
         piece = value.astype(jnp.bfloat16)
@@ -70,8 +74,8 @@
 
 def force_kernel(
     pairs_hbm, coords_hbm, displacement_hbm, bonds_hbm, out_ref,
-    listed, plan, ends_ref, lanes, coords, displacement, edge_out, edge_in, bonds, mask, owned, folded,
-    features, columns, wide_ref, wide_now, rows_ref, near, inverse, pulls, gains, back_strip, back_edge,
+    listed, plan, ends_ref, lanes, coords, displacement, edge_out, edge_in, bonds, reach, owned, folded,
+    features, columns, wide_ref, wide_now, rows_ref, near, inverse, steep, pulls, gains, back_strip, back_edge,
     from_strip, from_edge,
     in_sem, plan_sem, load_sem, halo_send, halo_recv, edge_send, edge_recv, back_send, back_recv,
     back_edge_send, back_edge_recv,
@@ -83,9 +87,22 @@
     group = pair_count // groups
     half = points // 2
     batches = per // BLOCK
+    wholes = -(-per // half)
     strip, tile = lax.axis_index("strip"), lax.axis_index("tile")
     strips, tiles = lax.axis_size("strip"), lax.axis_size("tile")
     strip_tiles = per * tiles
+
+    def exists(es, et):
+        s, t = strip + es, tile + et
+        return (s >= 0) & (s < strips) & (t >= 0) & (t < tiles)
+
+    barrier = pltpu.get_barrier_semaphore()
+    for es, et in AROUND:
+        @pl.when(exists(es, et))
+        def _(es=es, et=et):
+            pl.semaphore_signal(
+                barrier, inc=1, device_id=(strip + es, tile + et), device_id_type=MESH
+            )
 
     own = pl.ds(0, per)
     inputs = [
@@ -103,19 +120,6 @@
     for g in range(groups):
         load(g).start()
 
-    def exists(es, et):
-        s, t = strip + es, tile + et
-        return (s >= 0) & (s < strips) & (t >= 0) & (t < tiles)
-
-    around = EDGES + tuple((es, 0) for es in SIDES)
-    barrier = pltpu.get_barrier_semaphore()
-    for es, et in around:
-        @pl.when(exists(es, et))
-        def _(es=es, et=et):
-            pl.semaphore_signal(
-                barrier, inc=1, device_id=(strip + es, tile + et), device_id_type=MESH
-            )
-
     def remote(source, target, send, recv, es, et):
         return pltpu.make_async_remote_copy(
             src_ref=source, dst_ref=target, send_sem=send, recv_sem=recv,
@@ -170,7 +174,7 @@
     place, first, slot, across, main = locate(ends[0:1], ends[1:2], strip, tile, strip_tiles, per)
     step = jnp.where(across == 1, 1, DIGITS) * (DIGITS - 1)
     entries = (
-        slot, place, across * batches + first // BLOCK, lax.rem(first, BLOCK) * BLOCK,
+        slot, place, across * wholes + first // half, lax.rem(first, half),
         jnp.where(main == 1, step, points - step), 2 * across + main,
         (2 * across + main) * per + first, (2 * across + 1 - main) * per + first,
         across * per + first,
@@ -217,7 +221,7 @@
 
     def fold(g, carry):
         rows = owned[pl.ds(g * BLOCK, BLOCK)].reshape(BLOCK * BLOCK, points)
-        pieces = pieces_of(rows)
+        pieces = pieces_of(rows, 3)
         for across in range(2):
             parts = [dot_rows(piece, picks[across]) for piece in pieces]
             ordered = parts[0] + (parts[1] + parts[2])
@@ -231,20 +235,12 @@
                     [high.reshape(BLOCK, BLOCK, points), (twice - high).reshape(BLOCK, BLOCK, points)], axis=1
                 )
                 features[pl.ds((2 * across + h) * per + g * BLOCK, BLOCK)] = both.astype(jnp.bfloat16)
-            flat = jnp.concatenate([ordered, turned], axis=0).T
-            columns[across * batches + g] = flat[:half]
         return carry
 
     planned = pltpu.make_async_copy(listed, plan, plan_sem)
     planned.start()
     lax.fori_loop(0, batches, fold, 0, unroll=batches)
 
-    pl.semaphore_wait(barrier, sum(jnp.where(exists(es, et), 1, 0) for es, et in around))
-    each_edge(lambda i: edge(i).start(), False)
-    each_side(lambda i: halo(0, i).start(), False)
-    each_side(lambda i: halo(1, i).start(), False)
-    planned.wait()
-
     def merge(value, moved, shift):
         return jnp.where(moved, pltpu.roll(value, shift, 1), value)
 
@@ -254,16 +250,20 @@
 
     pieces_count = half // BLOCK
 
+    def widen(k, offset, target):
+        which, index = plan[2, k], lanes[plan[5, k]] + plan[3, k]
+        for c in range(3):
+            for j in range(pieces_count):
+                part = pl.ds(j * BLOCK, BLOCK)
+                target[k, c, part, :] = jnp.take_along_axis(columns[which, offset + c, part, :], index, axis=1)
+
+    def prepare_now(k, carry):
+        widen(k, 0, wide_now)
+        return carry
+
     def prepare(k, carry):
-        which, base, kind, shift = plan[2, k], plan[3, k], plan[5, k], plan[4, k]
-        index = lanes[kind] + base
-        sources = [columns[which, j * BLOCK : (j + 1) * BLOCK, :] for j in range(pieces_count)]
-        for c in range(3):
-            for offset, target in ((4, wide_ref), (0, wide_now)):
-                for j, source in enumerate(sources):
-                    target[k, c, j * BLOCK : (j + 1) * BLOCK, :] = jnp.take_along_axis(
-                        source, index + (offset + c), axis=1
-                    )
+        kind, shift = plan[5, k], plan[4, k]
+        widen(k, 4, wide_ref)
         moved = moved_of(kind)
         is_across = jnp.full((BLOCK, points), kind // 2) == 1
         is_odd = jnp.full((BLOCK, points), lax.rem(kind, 2)) == 1
@@ -282,27 +282,53 @@
         packed = pltpu.roll(packed, shift, 1)
         for j, large in enumerate(larges):
             held = jnp.where(moved, packed & (1 << j), large)
-            mask[k, j * BLOCK : (j + 1) * BLOCK] = jnp.where(held != 0, scale, 0.0)
-        return carry
-
-    def by_group(step, size):
+            reach[k, j * BLOCK : (j + 1) * BLOCK] = jnp.where(held != 0, horizon, 0.0)
+        return carry
+
+    def by_group(step, size, begin=0, end=pair_count):
         def run(g, carry):
             return lax.fori_loop(0, size, lambda i, c: step(g * size + i, c), carry, unroll=size)
 
-        lax.fori_loop(0, pair_count // size, run, 0)
+        lax.fori_loop(begin // size, end // size, run, 0)
+
+    for across in range(2):
+        for b in range(wholes):
+            count = min(half, per - b * half)
+            for c in range(BLOCK):
+                if c in (3, 7):
+                    continue
+                ordered = folded[pl.ds(across * per + b * half, count), c, :]
+                if count < half:
+                    ordered = jnp.concatenate([ordered, jnp.zeros((half - count, points), jnp.float32)], axis=0)
+                turned = pltpu.roll(ordered, half, 1)
+                columns[across * wholes + b, c] = jnp.concatenate([ordered, turned], axis=0).T[:half]
+
+    planned.wait()
+    pl.semaphore_wait(barrier, sum(jnp.where(exists(es, et), 1, 0) for es, et in AROUND))
+    each_edge(lambda i: edge(i).start(), False)
+    each_side(lambda i: halo(0, i).start(), False)
+    each_side(lambda i: halo(1, i).start(), False)
 
     for g in range(groups):
         load(g).wait()
-    by_group(prepare, math.gcd(pair_count, 8))
+    large_group = math.gcd(pair_count, 16)
+    ahead = large_group * AHEAD
+    apiece = pair_count // ahead
+
+    def prepare_some(k, carry):
+        for i in range(apiece):
+            prepare(apiece * k + i, carry)
+        prepare_now(k, carry)
+        return carry
+
+    by_group(prepare_some, STEP, 0, ahead)
 
     def unpack_edges(which):
         table = (coords, displacement)[which]
         for i, (es, et) in enumerate(EDGES):
-            @pl.when(exists(es, et))
-            def _(i=i):
-                for c in range(3):
-                    at = 3 * per + i
-                    table[c, at : at + 1, :] = edge_in[i, 3 * which + c : 3 * which + c + 1, :]
+            for c in range(3):
+                at = 3 * per + i
+                table[c, at : at + 1, :] = edge_in[i, 3 * which + c : 3 * which + c + 1, :]
 
     each_edge(lambda i: edge(i).wait_recv(), True)
     unpack_edges(0)
@@ -329,10 +355,20 @@
             ref2 = norm2(*(spread(rows, c) - wide_ref[k, c, part, :] for c in range(3)))
             inv_ref = lax.rsqrt(ref2)
             inverse[k, part] = inv_ref
-            near[k, part] = jnp.maximum(0.0, horizon - ref2 * inv_ref) * mask[k, part]
-        return carry
-
-    by_group(refer, math.gcd(pair_count, 16))
+            steep[k, part] = inv_ref * (1.0 / span)
+            near[k, part] = jnp.maximum(0.0, reach[k, part] - ref2 * inv_ref)
+        return carry
+
+    left = (pair_count - ahead) * large_group // pair_count
+    each = large_group // left
+
+    def refer_some(k, carry):
+        for i in range(each):
+            refer(each * k + i, carry)
+        prepare_now(ahead + k, carry)
+        return carry
+
+    by_group(refer_some, 2 * left, 0, pair_count - ahead)
 
     each_side(lambda i: halo(1, i).wait_recv(), True)
 
@@ -347,7 +383,7 @@
             part = pl.ds(at, chunk)
             now2 = norm2(*(spread(rows, c) - wide_now[k, c, part, :] for c in range(3)))
             inv_now, inv_ref = lax.rsqrt(now2), inverse[k, part]
-            soften = jnp.clip((1.0 + final_stretch) - now2 * inv_now * inv_ref, 0.0, span)
+            soften = jnp.clip((1.0 + final_stretch) / span - now2 * inv_now * steep[k, part], 0.0, 1.0)
             pull = (inv_ref - inv_now) * near[k, part] * soften
             lead = pull.astype(jnp.bfloat16)
             leads.append(lead)
@@ -364,12 +400,12 @@
             gains[c, pl.ds(k, 1), :] = gain[c : c + 1]
         return carry
 
-    by_group(act, math.gcd(pair_count, 32))
+    by_group(act, math.gcd(pair_count, 64))
 
     def row_pieces():
         pieces = []
         for c in range(3):
-            pieces += pieces_of(gains[c])
+            pieces += pieces_of(scale * gains[c], PIECES)
         return jnp.concatenate(pieces, axis=1)
 
     def gather(start, count, listed, pieces):
@@ -378,18 +414,17 @@
         sums = dot_rows(weight, pieces)
         totals = []
         for c in range(3):
-            parts = [sums[:, (3 * c + j) * points : (3 * c + j + 1) * points] for j in range(3)]
-            totals.append(parts[0] + (parts[1] + parts[2]))
+            at = PIECES * c * points
+            totals.append(sums[:, at : at + points] + sums[:, at + points : at + PIECES * points])
         return totals
 
     second_pieces = row_pieces()
-    for c, total in enumerate(gather(3 * per, BLOCK, second_ends, second_pieces)):
+    for c, total in enumerate(gather(per, 2 * per + BLOCK, second_ends, second_pieces)):
+        for i in range(len(SIDES)):
+            back_strip[i, c] = total[i * per : (i + 1) * per]
         for i in range(len(EDGES)):
-            back_edge[i, c : c + 1, :] = total[i : i + 1]
+            back_edge[i, c : c + 1, :] = total[2 * per + i : 2 * per + i + 1]
     each_edge(lambda i: edge_back(i).start(), False)
-    for i, es in enumerate(SIDES):
-        for c, total in enumerate(gather(STRIPS.index(es) * per, per, second_ends, second_pieces)):
-            back_strip[i, c] = total
     each_side(lambda i: back(i).start(), False)
     for c, total in enumerate(gather(0, per, second_ends, second_pieces)):
         out_ref[c] = total
@@ -421,8 +456,12 @@
     unfold = jnp.concatenate(picks, axis=1)
     for c in range(3):
         both = jnp.concatenate([sums[0][c], sums[1][c]], axis=1)
-        parts = [dot_columns(piece, unfold) for piece in pieces_of(both)]
-        out_ref[c] += parts[0] + (parts[1] + parts[2])
+        parts = [dot_columns(piece, unfold) for piece in pieces_of(both, PIECES)]
+        out_ref[c] += parts[0] + parts[1]
+
+    for which in range(2):
+        each_side(lambda i: halo(which, i).wait_send(), False)
+    each_edge(lambda i: edge(i).wait_send(), False)
 
     def receive_edge(i):
         es, et = EDGES[i]
@@ -437,9 +476,6 @@
 
     each_edge(receive_edge, True)
     each_side(receive, True)
-    for which in range(2):
-        each_side(lambda i: halo(which, i).wait_send(), False)
-    each_edge(lambda i: edge(i).wait_send(), False)
     each_edge(lambda i: edge_back(i).wait_send(), False)
     each_side(lambda i: back(i).wait_send(), False)
 
@@ -450,7 +486,7 @@
     groups = math.gcd(pair_count, 8)
     slots = 3 * per + BLOCK
     half = points // 2
-    batches = per // BLOCK
+    wholes = -(-per // half)
     f32 = jnp.float32
     hbm = pl.BlockSpec(memory_space=pltpu.HBM)
     total = pl.pallas_call(
@@ -472,10 +508,11 @@
             pltpu.VMEM((per, BLOCK, points), f32),
             pltpu.VMEM((2 * per, BLOCK, points), f32),
             pltpu.VMEM((4 * per, 2 * BLOCK, points), jnp.bfloat16),
-            pltpu.VMEM((2 * batches, half, points), f32),
+            pltpu.VMEM((2 * wholes, BLOCK, half, points), f32),
             pltpu.VMEM((pair_count, 3, half, points), f32),
             pltpu.VMEM((pair_count, 3, half, points), f32),
             pltpu.VMEM((pair_count, BLOCK, points), f32),
+            pltpu.VMEM((pair_count, half, points), f32),
             pltpu.VMEM((pair_count, half, points), f32),
             pltpu.VMEM((pair_count, half, points), f32),
             pltpu.VMEM((pair_count, points, points), jnp.bfloat16),

time: 18.2 us -> 17.6 us (0.967)
  Pallas kernels: 17.4 us -> 16.8 us
    pallas_call x1, Pallas kernels: 17.4 us -> 16.8 us  [on_device(): pl.pallas_call(force_kernel, in_specs=[hbm] * 4, out_specs=pl.BlockSpec(m...]
where the time goes in v3:
time: 17.6 us; the launch traced here: 17.4 us
  Pallas kernels  16.8 us (95%)
  local copies, waits for them, and re-layouts  0.64 us (4%)
    pallas_call x1, Pallas kernels, on_device(): pl.pallas_call(force_kernel, in_specs=[hbm] * 4, out_specs=pl.BlockSpec(m...  16.8 us
    unnamed x1, local copies, waits for them, and re-layouts  0.64 us

profile of v3, /device:TPU:0, one launch (start us, length us, event | category | flops | bytes accessed | tf_op | source)
XLA Modules:
  0.0 17.4 jit_solution(5176859412769180289)
XLA Ops:
  0.0 16.8 %shard_map.46 = f32[3,48,128]{2,1,0:T(8,128)S(1)} custom-call(s32[2,64]{1,0:T(2,128)} %bitcast.7, f32[3,48,128]{2,1,0:T(8,128)} %bitcast.5, f32[3,48,128]{2,1,0:T(8,128)} %bitcast.6, s32[64,128,128]{2,1,0:T(8,128)} %bonds_hbm.1), custom_call_target="tpu_custom_call" | custom-call | tf_op jit(solution)/shard_map/pallas_call | solution.py:492
  16.8 0.6 %copy.6 = f32[48,3,128]{2,0,1:T(8,128)} copy(f32[48,3,128]{2,0,1:T(8,128)S(1)} %bitcast.4) | data formatting | bytes 147456

commit v4 on v3

--- a/solution.py
+++ b/solution.py
@@ -190,6 +190,13 @@
             edge_out[i, c : c + 1, :] = coords[c, at : at + 1, :]
             edge_out[i, 3 + c : 4 + c, :] = displacement[c, at : at + 1, :]
 
+    planned = pltpu.make_async_copy(listed, plan, plan_sem)
+    planned.start()
+    pl.semaphore_wait(barrier, sum(jnp.where(exists(es, et), 1, 0) for es, et in AROUND))
+    each_edge(lambda i: edge(i).start(), False)
+    each_side(lambda i: halo(0, i).start(), False)
+    each_side(lambda i: halo(1, i).start(), False)
+    planned.wait()
     places = lax.broadcasted_iota(jnp.int32, (per, points), 0) + tile * per
     bases = (
         (DIGITS * strip).astype(jnp.float32) + CENTRE[0],
@@ -237,9 +244,6 @@
                 features[pl.ds((2 * across + h) * per + g * BLOCK, BLOCK)] = both.astype(jnp.bfloat16)
         return carry
 
-    planned = pltpu.make_async_copy(listed, plan, plan_sem)
-    planned.start()
-    lax.fori_loop(0, batches, fold, 0, unroll=batches)
 
     def merge(value, moved, shift):
         return jnp.where(moved, pltpu.roll(value, shift, 1), value)
@@ -291,6 +295,7 @@
 
         lax.fori_loop(begin // size, end // size, run, 0)
 
+    lax.fori_loop(0, batches, fold, 0, unroll=batches)
     for across in range(2):
         for b in range(wholes):
             count = min(half, per - b * half)
@@ -303,11 +308,6 @@
                 turned = pltpu.roll(ordered, half, 1)
                 columns[across * wholes + b, c] = jnp.concatenate([ordered, turned], axis=0).T[:half]
 
-    planned.wait()
-    pl.semaphore_wait(barrier, sum(jnp.where(exists(es, et), 1, 0) for es, et in AROUND))
-    each_edge(lambda i: edge(i).start(), False)
-    each_side(lambda i: halo(0, i).start(), False)
-    each_side(lambda i: halo(1, i).start(), False)
 
     for g in range(groups):
         load(g).wait()

time: 17.6 us -> 17.2 us (0.977)
  Pallas kernels: 16.8 us -> 16.4 us
    pallas_call x1, Pallas kernels: 16.8 us -> 16.4 us  [on_device(): pl.pallas_call(force_kernel, in_specs=[hbm] * 4, out_specs=pl.BlockSpec(m...]
where the time goes in v4:
time: 17.2 us; the launch traced here: 17 us
  Pallas kernels  16.4 us (95%)
  local copies, waits for them, and re-layouts  0.64 us (4%)
    pallas_call x1, Pallas kernels, on_device(): pl.pallas_call(force_kernel, in_specs=[hbm] * 4, out_specs=pl.BlockSpec(m...  16.4 us
    unnamed x1, local copies, waits for them, and re-layouts  0.64 us

profile of v4, /device:TPU:0, one launch (start us, length us, event | category | flops | bytes accessed | tf_op | source)
XLA Modules:
  0.0 17.0 jit_solution(6985599929960899590)
XLA Ops:
  0.0 16.4 %shard_map.46 = f32[3,48,128]{2,1,0:T(8,128)S(1)} custom-call(s32[2,64]{1,0:T(2,128)} %bitcast.7, f32[3,48,128]{2,1,0:T(8,128)} %bitcast.5, f32[3,48,128]{2,1,0:T(8,128)} %bitcast.6, s32[64,128,128]{2,1,0:T(8,128)} %bonds_hbm.1), custom_call_target="tpu_custom_call" | custom-call | tf_op jit(solution)/shard_map/pallas_call | solution.py:492
  16.4 0.6 %copy.6 = f32[48,3,128]{2,0,1:T(8,128)} copy(f32[48,3,128]{2,0,1:T(8,128)S(1)} %bitcast.4) | data formatting | bytes 147456

commit v5 on v4

--- a/solution.py
+++ b/solution.py
@@ -419,12 +419,13 @@
         return totals
 
     second_pieces = row_pieces()
-    for c, total in enumerate(gather(per, 2 * per + BLOCK, second_ends, second_pieces)):
+    for c, total in enumerate(gather(3 * per, BLOCK, second_ends, second_pieces)):
+        for i in range(len(EDGES)):
+            back_edge[i, c : c + 1, :] = total[i : i + 1]
+    each_edge(lambda i: edge_back(i).start(), False)
+    for c, total in enumerate(gather(per, 2 * per, second_ends, second_pieces)):
         for i in range(len(SIDES)):
             back_strip[i, c] = total[i * per : (i + 1) * per]
-        for i in range(len(EDGES)):
-            back_edge[i, c : c + 1, :] = total[2 * per + i : 2 * per + i + 1]
-    each_edge(lambda i: edge_back(i).start(), False)
     each_side(lambda i: back(i).start(), False)
     for c, total in enumerate(gather(0, per, second_ends, second_pieces)):
         out_ref[c] = total

time: 17.2 us -> 17.1 us (level)
  no operation moved by 1% of the time
where the time goes in v5:
time: 17.1 us; the launch traced here: 17 us
  Pallas kernels  16.3 us (95%)
  local copies, waits for them, and re-layouts  0.64 us (4%)
    pallas_call x1, Pallas kernels, on_device(): pl.pallas_call(force_kernel, in_specs=[hbm] * 4, out_specs=pl.BlockSpec(m...  16.3 us
    unnamed x1, local copies, waits for them, and re-layouts  0.64 us

profile of v5, /device:TPU:0, one launch (start us, length us, event | category | flops | bytes accessed | tf_op | source)
XLA Modules:
  0.0 17.0 jit_solution(2700479024782472969)
XLA Ops:
  0.0 16.3 %shard_map.46 = f32[3,48,128]{2,1,0:T(8,128)S(1)} custom-call(s32[2,64]{1,0:T(2,128)} %bitcast.7, f32[3,48,128]{2,1,0:T(8,128)} %bitcast.5, f32[3,48,128]{2,1,0:T(8,128)} %bitcast.6, s32[64,128,128]{2,1,0:T(8,128)} %bonds_hbm.1), custom_call_target="tpu_custom_call" | custom-call | tf_op jit(solution)/shard_map/pallas_call | solution.py:493
  16.3 0.6 %copy.6 = f32[48,3,128]{2,0,1:T(8,128)} copy(f32[48,3,128]{2,0,1:T(8,128)S(1)} %bitcast.4) | data formatting | bytes 147456
